TPU v7x, 32 devices: a whole 2x2x4 slice. The times are simulated.
32 devices in a mesh: row: 4 (over y, x), col: 8 (over z, core).
Axes of the slice: x: 2, y: 2, z: 4, core: 2. Of those that a mesh axis runs over, the one named last changes fastest.
Arguments:
- model_gradient: float32 [3, 512, 512, 256], P(None, 'row', 'col'), may hold values from -6 to 6
- filter_x: float32 [512, 512], replicated, may hold values from 0 to 1, as said below
- filter_y: float32 [512, 512], replicated, may hold values from 0 to 1, as said below
- filter_z: float32 [256, 256], replicated, may hold values from 0 to 1, as said below
- depth_scale: float32 [3, 256], replicated, may hold values from 0.3 to 3
Outputs:
- smoothed: float32 [3, 512, 512, 256], P(None, 'row', 'col')
Inputs may be any that keep to these rules, and one draw needn't show every extreme that they name: `filter_x`: each row is a nonnegative smoothing kernel of its own width plus one half on the diagonal; rows sum to one. `filter_y`: each row is a nonnegative smoothing kernel of its own width plus one half on the diagonal; rows sum to one. `filter_z`: each row is a nonnegative smoothing kernel of its own width plus one half on the diagonal; rows sum to one.
All inputs are finite; a program needn't handle non-finite values.
Results may differ from a plain program's by a relative error of at most 0.0001.
Values sent between devices are 32-bit elements; how exact they have to be, the bound alone decides.
A program may use at most 192 MiB of HBM per device.

v0:
```python
import jax
import jax.numpy as jnp
from jax import lax
from jax.sharding import PartitionSpec as P


def plane_filter(incoming_part, filter_x, filter_y, rows, cols):
    highest_accuracy = lax.Precision.HIGHEST
    params, xloc, yloc = (incoming_part.shape[0], incoming_part.shape[1], incoming_part.shape[2])
    matrix_x = filter_x.reshape(rows, xloc, rows, xloc)
    lateral_y_matrix = filter_y.reshape(cols, yloc, cols, yloc)
    partial_value = jnp.einsum(
        "ABRa,pabRSz->ABpbSz", matrix_x, incoming_part, precision=highest_accuracy
    )
    return jnp.einsum(
        "CDSb,ABpbSz->ACpBDz", lateral_y_matrix, partial_value, precision=highest_accuracy
    )


def shards(model_gradient, filter_x, filter_y, filter_z, depth_scale):
    highest_accuracy = lax.Precision.HIGHEST
    rows = lax.axis_size("row")
    cols = lax.axis_size("col")
    params, xloc, yloc, depth = model_gradient.shape
    scaled_filter = depth_scale[:, :, None] * filter_z[None, :, :]
    column_first = jnp.einsum(
        "pkz,pabz->pabk", scaled_filter, model_gradient, precision=highest_accuracy
    )
    depth_block = depth // (rows * cols)
    outgoing = column_first.reshape(params, xloc, yloc, rows * cols, depth_block)
    incoming_part = lax.all_to_all(
        outgoing, ("row", "col"), split_axis=3, concat_axis=3, tiled=True
    )
    incoming_part = incoming_part.reshape(params, xloc, yloc, rows, cols, depth_block)
    planes = plane_filter(incoming_part, filter_x, filter_y, rows, cols)
    planes = planes.reshape(rows * cols, params, xloc, yloc, depth_block)
    result = lax.all_to_all(planes, ("row", "col"), split_axis=0, concat_axis=4, tiled=True)
    return result.reshape(params, xloc, yloc, depth)


def solution(mesh):
    return jax.shard_map(
        shards,
        mesh=mesh,
        in_specs=(P(None, "row", "col", None), P(), P(), P(), P()),
        out_specs=P(None, "row", "col", None),
        check_vma=False,
    )
```

profile of v0, /device:TPU:0, one launch (start us, length us, event | category | flops | bytes accessed | tf_op | source)
XLA Modules:
  0.0 1324.2 jit_solution(16032111369222720225)
XLA Ops:
  0.0 44.2 %fusion.7 = f32[3,128,64,32,8]{1,4,3,2,0:T(8,128)} fusion(f32[3,128,64,256]{3,2,1,0:T(8,128)} %param.5, f32[256,256]{1,0:T(8,128)} %param.8, f32[3,256]{1,0:T(4,128)} %param.9), kind=kOutput, calls=%fused_computation.8 | convolution fusion | flops 19327549440 | bytes 50596864 | tf_op jit(solution)/shard_map/pkz,pabz->pabk/dot_general | solution.py:26
  44.2 17.2 %copy.21 = f32[3,128,64,32,8]{1,4,2,0,3:T(8,128)} copy(f32[3,128,64,32,8]{1,4,3,2,0:T(8,128)} %fusion.7) | data formatting | bytes 50331648 | tf_op jit(solution)/shard_map/reshape | solution.py:30
  61.4 0.0 copy-start
  61.4 7.6 all-to-all-start
  69.0 0.0 copy-done
  69.0 0.4 reshape.23
  69.4 1.6 reshape.24
  71.0 542.2 %all-to-all-done = f32[3,128,64,32,8]{1,4,2,0,3:T(8,128)} async-done(((f32[3,128,64,32,8]{1,4,2,0,3:T(8,128)}), f32[3,128,64,32,8]{1,4,2,0,3:T(8,128)}, u32[]{:S(2)}, u32[]{:S(2)}) %all-to-all-start) | async-done | bytes 25165856 | tf_op jit(solution)/shard_map/all_to_all | solution.py:31
  613.2 49.8 %fusion.2 = f32[3,64,8,8,4,128,1]{5,1,6,2,3,0,4:T(8,128)S(1)} fusion(f32[3,128,64,4,8,8]{1,5,2,0,4,3:T(8,128)} %bitcast.4, f32[4,128,4,128,1,1,1]{3,2,1,0,6,5,4:T(4,128)S(1)} %bitcast.41), kind=kOutput, calls=%fused_computation.2 | convolution fusion | flops 38654705664 | bytes 51380224 | tf_op jit(solution)/shard_map/ABRa,pabRSz->ABpbSz/dot_general | solution.py:12
  663.0 45.9 %fusion.10 = f32[4,8,3,128,64,8]{3,4,1,5,2,0:T(8,128)} fusion(f32[3,64,8,8,4,128,1]{5,1,6,2,3,0,4:T(8,128)S(1)} %fusion.2, f32[8,64,8,64,1,1,1]{3,2,1,0,6,5,4:T(8,128)S(1)} %bitcast.42), kind=kOutput, calls=%fused_computation.9 | convolution fusion | flops 38654705664 | bytes 51380224 | tf_op jit(solution)/shard_map/CDSb,ABpbSz->ACpBDz/dot_general | solution.py:15
  708.9 26.2 %copy.26 = f32[4,8,3,128,64,8]{3,5,4,2,1,0:T(8,128)S(1)} copy(f32[4,8,3,128,64,8]{3,4,1,5,2,0:T(8,128)} %fusion.10) | data formatting | bytes 50331648 | tf_op jit(solution)/shard_map/CDSb,ABpbSz->ACpBDz/transpose | solution.py:15
  735.1 547.0 %all_to_all.20 = f32[32,3,128,64,8]{2,4,3,1,0:T(8,128)} all-to-all(f32[32,3,128,64,8]{2,4,3,1,0:T(8,128)S(1)} %bitcast.40), channel_id=1, replica_groups=mesh['row'=4,'col'=8] {'row','col'}, dimensions={0} | all-to-all | bytes 50331648 | tf_op jit(solution)/shard_map/all_to_all | solution.py:37
  1282.1 17.4 %copy_bitcast_fusion = f32[3,128,64,256]{1,3,2,0:T(8,128)} fusion(f32[32,3,128,64,8]{2,4,3,1,0:T(8,128)} %all_to_all.20), kind=kLoop, calls=%fused_computation.5 | loop fusion | bytes 50331648 | tf_op jit(solution)/shard_map/reshape | solution.py:38
  1299.5 24.7 %copy.28 = f32[3,128,64,256]{3,2,1,0:T(8,128)} copy(f32[3,128,64,256]{1,3,2,0:T(8,128)} %copy_bitcast_fusion) | data formatting | bytes 50331648 | tf_op jit(solution)/shard_map/reshape | solution.py:38
Async XLA Ops:
  61.4 7.6 copy-start
  61.4 551.8 %all-to-all-start = ((f32[3,128,64,32,8]{1,4,2,0,3:T(8,128)}), f32[3,128,64,32,8]{1,4,2,0,3:T(8,128)}, u32[]{:S(2)}, u32[]{:S(2)}) async-start(f32[3,128,64,32,8]{1,4,2,0,3:T(8,128)} %copy.21), calls=%async_computation | async-start | bytes 50331648 | tf_op jit(solution)/shard_map/all_to_all | solution.py:31
where the time goes:
time: 1320 us
  blocking collectives  547 us (41%)
  waiting for transfers between devices  542 us (41%)
  matrix products  140 us (11%)
  local copies, waits for them, and re-layouts  87.5 us (7%)
    all_to_all x1, blocking collectives, shards(): lax.all_to_all(planes, ('row', 'col'), split_axis=0, concat_axis=4, tiled...  547 us
    all_to_all x1, waiting for transfers between devices, shards(): lax.all_to_all(outgoing, ('row', 'col'), split_axis=3, concat_axis=3, til...  542 us
    dot_general x1, matrix products, plane_filter(): jnp.einsum('ABRa,pabRSz->ABpbSz', matrix_x, incoming_part, precision=high...  49.8 us
    dot_general x1, matrix products, plane_filter(): jnp.einsum('CDSb,ABpbSz->ACpBDz', lateral_y_matrix, partial_value, precis...  45.9 us
    dot_general x1, matrix products, shards(): jnp.einsum('pkz,pabz->pabk', scaled_filter, model_gradient, precision=hig...  44.2 us
    reshape x2, local copies, waits for them, and re-layouts, shards(): return result.reshape(params, xloc, yloc, depth)  42.1 us
  transfers between devices with their start and end apart: 1, of which 1 were waited for; matrix products, arithmetic and copies ran while one was open for 0% of the time, Pallas kernels for 0%

commit v1 on v0

--- a/solution.py
+++ b/solution.py
@@ -28,8 +28,14 @@
     )
     depth_block = depth // (rows * cols)
     outgoing = column_first.reshape(params, xloc, yloc, rows * cols, depth_block)
-    incoming_part = lax.all_to_all(
-        outgoing, ("row", "col"), split_axis=3, concat_axis=3, tiled=True
+    incoming_part = jnp.concatenate(
+        lax.all_to_all(
+            jnp.stack(jnp.split(outgoing, lax.axis_size(("row", "col")), axis=3)),
+            ("row", "col"),
+            0,
+            0,
+        ),
+        axis=3,
     )
     incoming_part = incoming_part.reshape(params, xloc, yloc, rows, cols, depth_block)
     planes = plane_filter(incoming_part, filter_x, filter_y, rows, cols)

time: 1320 us -> 1380 us (1.045)
  local copies, waits for them, and re-layouts: 87.5 us -> 137 us
    unnamed x2 -> x33, local copies, waits for them, and re-layouts: 0.01 us -> 64.5 us
    reshape x1 -> x0, local copies, waits for them, and re-layouts: 17.2 us -> none  [shards(): column_first.reshape(params, xloc, yloc, rows * cols, depth_block)]
where the time goes in v1:
time: 1380 us; the launch traced here: 1370 us
  blocking collectives  547 us (40%)
  waiting for transfers between devices  542 us (39%)
  matrix products  140 us (10%)
  local copies, waits for them, and re-layouts  137 us (10%)
    all_to_all x1, blocking collectives, shards(): lax.all_to_all(planes, ('row', 'col'), split_axis=0, concat_axis=4, tiled...  547 us
    all_to_all x1, waiting for transfers between devices, shards(): lax.all_to_all(jnp.stack(jnp.split(outgoing, lax.axis_size(('row', 'col')...  542 us
    unnamed x33, local copies, waits for them, and re-layouts  64.5 us
    dot_general x1, matrix products, plane_filter(): jnp.einsum('ABRa,pabRSz->ABpbSz', matrix_x, incoming_part, precision=high...  49.8 us
    dot_general x1, matrix products, plane_filter(): jnp.einsum('CDSb,ABpbSz->ACpBDz', lateral_y_matrix, partial_value, precis...  45.9 us
    dot_general x1, matrix products, shards(): jnp.einsum('pkz,pabz->pabk', scaled_filter, model_gradient, precision=hig...  44.2 us
    reshape x2, local copies, waits for them, and re-layouts, shards(): return result.reshape(params, xloc, yloc, depth)  42.1 us
  transfers between devices with their start and end apart: 1, of which 1 were waited for; matrix products, arithmetic and copies ran while one was open for 0% of the time, Pallas kernels for 0%

profile of v1, /device:TPU:0, one launch (start us, length us, event | category | flops | bytes accessed | tf_op | source)
XLA Modules:
  0.0 1373.6 jit_solution(7435603772383771790)
XLA Ops:
  0.0 44.2 %fusion.6 = f32[3,128,64,32,8]{1,4,3,2,0:T(8,128)} fusion(f32[3,128,64,256]{3,2,1,0:T(8,128)} %param.5, f32[256,256]{1,0:T(8,128)} %param.8, f32[3,256]{1,0:T(4,128)} %param.9), kind=kOutput, calls=%fused_computation.7 | convolution fusion | flops 19327549440 | bytes 50596864 | tf_op jit(solution)/shard_map/pkz,pabz->pabk/dot_general | solution.py:26
  44.2 2.1 fusion.45
  46.3 2.1 fusion.44
  54.6 2.1 fusion.40
  56.7 2.1 fusion.39
  65.0 2.1 fusion.35
  69.2 2.1 fusion.33
  71.2 2.1 fusion.32
  75.4 2.1 fusion.30
  79.6 2.1 fusion.28
  83.7 2.1 fusion.26
  87.9 2.1 fusion.24
  92.1 2.1 fusion.22
  94.2 2.1 fusion.21
  102.4 2.1 fusion.17
  104.5 2.1 fusion.16
  110.8 7.4 all-to-all-start
  120.2 542.4 %all-to-all-done = f32[32,3,128,64,1,8]{2,5,3,1,4,0:T(8,128)} async-done(((f32[32,3,128,64,1,8]{2,5,3,1,4,0:T(8,128)}), f32[32,3,128,64,1,8]{2,5,3,1,4,0:T(8,128)}, u32[]{:S(2)}, u32[]{:S(2)}) %all-to-all-start) | async-done | bytes 25165856 | tf_op jit(solution)/shard_map/all_to_all | solution.py:32
  662.5 49.8 %fusion.2 = f32[3,64,8,8,4,128,1]{5,1,6,2,3,0,4:T(8,128)S(1)} fusion(f32[3,128,64,4,8,8,1]{1,5,2,0,4,3,6:T(8,128)} %bitcast.39, f32[4,128,4,128,1,1,1]{3,2,1,0,4,5,6:T(4,128)S(1)} %reshape.29), kind=kOutput, calls=%fused_computation.2 | convolution fusion | flops 38654705664 | bytes 51380224 | tf_op jit(solution)/shard_map/ABRa,pabRSz->ABpbSz/dot_general | solution.py:12
  712.4 45.9 %fusion.9 = f32[4,8,3,128,64,8]{3,4,1,5,2,0:T(8,128)} fusion(f32[3,64,8,8,4,128,1]{5,1,6,2,3,0,4:T(8,128)S(1)} %fusion.2, f32[8,64,8,64,1,1,1]{3,2,1,0,6,5,4:T(8,128)S(1)} %bitcast.231), kind=kOutput, calls=%fused_computation.8 | convolution fusion | flops 38654705664 | bytes 51380224 | tf_op jit(solution)/shard_map/CDSb,ABpbSz->ACpBDz/dot_general | solution.py:15
  758.3 26.2 %copy.72 = f32[4,8,3,128,64,8]{3,5,4,2,1,0:T(8,128)S(1)} copy(f32[4,8,3,128,64,8]{3,4,1,5,2,0:T(8,128)} %fusion.9) | data formatting | bytes 50331648 | tf_op jit(solution)/shard_map/CDSb,ABpbSz->ACpBDz/transpose | solution.py:15
  784.5 547.0 %all_to_all.20 = f32[32,3,128,64,8]{2,4,3,1,0:T(8,128)} all-to-all(f32[32,3,128,64,8]{2,4,3,1,0:T(8,128)S(1)} %bitcast.230), channel_id=1, replica_groups=mesh['row'=4,'col'=8] {'row','col'}, dimensions={0} | all-to-all | bytes 50331648 | tf_op jit(solution)/shard_map/all_to_all | solution.py:43
  1331.5 17.4 %copy_bitcast_fusion = f32[3,128,64,256]{1,3,2,0:T(8,128)} fusion(f32[32,3,128,64,8]{2,4,3,1,0:T(8,128)} %all_to_all.20), kind=kLoop, calls=%fused_computation.4 | loop fusion | bytes 50331648 | tf_op jit(solution)/shard_map/reshape | solution.py:44
  1348.8 24.7 %copy.74 = f32[3,128,64,256]{3,2,1,0:T(8,128)} copy(f32[3,128,64,256]{1,3,2,0:T(8,128)} %copy_bitcast_fusion) | data formatting | bytes 50331648 | tf_op jit(solution)/shard_map/reshape | solution.py:44
  (21 shorter events, 37.1 us)
Async XLA Ops:
  110.8 7.4 copy-start
  110.8 551.8 %all-to-all-start = ((f32[32,3,128,64,1,8]{2,5,3,1,4,0:T(8,128)}), f32[32,3,128,64,1,8]{2,5,3,1,4,0:T(8,128)}, u32[]{:S(2)}, u32[]{:S(2)}) async-start(f32[32,3,128,64,1,8]{2,5,3,1,4,0:T(8,128)} %fusion.14), calls=%async_computation | async-start | bytes 50331648 | tf_op jit(solution)/shard_map/all_to_all | solution.py:32
